TPU v7x, 32 devices: a whole 2x2x4 slice. The times are simulated.
32 devices in a mesh: sx: 4 (over x, core), sy: 4 (over z), dp: 2 (over y).
Axes of the slice: x: 2, y: 2, z: 4, core: 2. Of those that a mesh axis runs over, the one named last changes fastest.
Arguments:
- tokens: bfloat16 [2, 8192, 1280], P('dp', ('sx', 'sy')), may hold values from -6 to 6
- lengths: int32 [2, 64], P('dp'), may hold values from 1 to 512, 8192 in all within a row
- ln_gain: float32 [1280], replicated, may hold values from 0.1 to 1.9
- w_qkv: bfloat16 [1280, 3840], P('dp'), may hold values from -4 to 4, as said below
- w_out: bfloat16 [1280, 1280], P('dp'), may hold values from -0.15625 to 0.15625
Outputs:
- hidden: bfloat16 [2, 8192, 1280], P('dp', ('sx', 'sy'))
- pooled: float32 [2, 64, 1280], P('dp')
Inputs may be any that keep to these rules, and one draw needn't show every extreme that they name: The 64 lengths of a row sum to 8192; images are packed end to end in order. `w_qkv`: columns are queries, then keys, then values, each of 16 heads of 80 columns.
All inputs are finite; a program needn't handle non-finite values.
Results may differ from a plain program's by a relative error of at most 0.0051.
Values may be sent and summed in bfloat16 or wider, within the bound.
A program may use at most 128 MiB of HBM per device.

v0:
```python
import functools

import jax
import jax.numpy as jnp
from jax import lax
from jax.experimental import pallas as pl
from jax.experimental.pallas import tpu as pltpu
from jax.sharding import PartitionSpec as P

HEADS = 16
MAXLEN = 512
MESH = pl.DeviceIdType.MESH
CHUNKS = 5
HALO_CHUNKS = 2
QBLOCK = 256
KBLOCK = 256
LANES = 128
FAR = -1e30


def remote(src, dst, send, recv, device):
    return pltpu.make_async_remote_copy(
        src_ref=src, dst_ref=dst, send_sem=send, recv_sem=recv, device_id=device, device_id_type=MESH
    )


def project_kernel(
    nx, ny, tok, gain, wq, wo, q_out, k_out, v_out, wo_out,
    toks, normed, wq_full, wo_full,
    y_send, y_recv, x_send, x_recv, d_send, d_recv, h_send, h_recv, local_sem,
):
    sx, sy, dp = lax.axis_index("sx"), lax.axis_index("sy"), lax.axis_index("dp")
    chips = nx // 2
    chip, core = sx // 2, lax.rem(sx, 2)
    count = nx * ny
    shard = sx * ny + sy
    before, after = lax.rem(shard + count - 1, count), lax.rem(shard + 1, count)
    prev_id = (before // ny, lax.rem(before, ny), dp)
    next_id = (after // ny, lax.rem(after, ny), dp)
    y_id = (sx, sy, 1 - dp)
    partner = (chip * 2 + 1 - core, sy, dp)

    def chip_id(step):
        return (lax.rem(chip + step, chips) * 2 + core, sy, dp)

    local, width = tok.shape
    half = wq.shape[0]
    quarter = half // nx
    piece = quarter // CHUNKS

    def rows(owner, slot, j):
        return pl.ds(pl.multiple_of(owner * half + slot * quarter + j * piece, piece), piece)

    barrier = pltpu.get_barrier_semaphore()
    greeted = [prev_id, next_id, y_id, partner] + [chip_id(s) for s in range(1, chips)]
    for device in greeted:
        pl.semaphore_signal(barrier, inc=1, device_id=device, device_id_type=MESH)
    own_tokens = pltpu.make_async_copy(tok, toks.at[pl.ds(MAXLEN, local)], local_sem.at[0])
    own_q = pltpu.make_async_copy(wq, wq_full.at[pl.ds(pl.multiple_of(dp * half, half), half)], local_sem.at[1])
    own_o = pltpu.make_async_copy(wo, wo_full.at[pl.ds(pl.multiple_of(dp * half, half), half)], local_sem.at[2])
    own_tokens.start()
    own_q.start()
    own_o.start()
    pl.semaphore_wait(barrier, len(greeted))

    weights = ((wq, wq_full), (wo, wo_full))
    hop = MAXLEN // HALO_CHUNKS
    sends = []
    for w, (part, full) in enumerate(weights):
        for j in range(CHUNKS):
            copy = remote(
                part.at[pl.ds(pl.multiple_of(sx * quarter + j * piece, piece), piece)],
                full.at[rows(dp, sx, j)], y_send.at[w, j], y_recv.at[w, j], y_id,
            )
            copy.start()
            sends.append(copy)

    def up(j):
        return remote(
            tok.at[pl.ds(local - MAXLEN + j * hop, hop)], toks.at[pl.ds(j * hop, hop)],
            h_send.at[0, j], h_recv.at[0, j], next_id,
        )

    def down(j):
        return remote(
            tok.at[pl.ds(j * hop, hop)], toks.at[pl.ds(MAXLEN + local + j * hop, hop)],
            h_send.at[1, j], h_recv.at[1, j], prev_id,
        )

    first, last = shard == 0, shard == count - 1

    @pl.when(jnp.logical_not(last))
    def _():
        for j in range(HALO_CHUNKS):
            up(j).start()

    @pl.when(jnp.logical_not(first))
    def _():
        for j in range(HALO_CHUNKS):
            down(j).start()

    @pl.when(first)
    def _():
        toks[pl.ds(0, MAXLEN)] = jnp.zeros((MAXLEN, width), toks.dtype)

    @pl.when(last)
    def _():
        toks[pl.ds(MAXLEN + local, MAXLEN)] = jnp.zeros((MAXLEN, width), toks.dtype)

    def norm(start, size):
        step = 64

        @pl.loop(0, size // step)
        def _(i):
            where = pl.ds(pl.multiple_of(start + i * step, step), step)
            values = toks[where].astype(jnp.float32)
            center = values - jnp.mean(values, axis=-1, keepdims=True)
            spread = jnp.mean(center * center, axis=-1, keepdims=True)
            normed[where] = (center * lax.rsqrt(spread + 1e-05) * gain[...]).astype(normed.dtype)

    def project(start, size, out, out_start, which):
        cols = 256

        @pl.loop(0, width // cols)
        def _(c):
            at = pl.multiple_of(c * cols, cols)
            product = jnp.dot(
                normed[pl.ds(start, size)], wq_full[:, pl.ds(which * width + at, cols)],
                preferred_element_type=jnp.float32,
            )
            out[pl.ds(out_start, size), pl.ds(at, cols)] = product.astype(out.dtype)

    own_tokens.wait()
    norm(MAXLEN, local)

    def relay(w):
        full = weights[w][1]

        def pass_across(step, j):
            slot = lax.rem(chip + chips - step, chips) * 2 + core
            here = full.at[rows(1 - dp, slot, j)]
            if step == 0:
                remote(here, here, y_send.at[w, j], y_recv.at[w, j], y_id).wait_recv()
                for s in range(1, chips):
                    copy = remote(here, here, x_send.at[w, s - 1, j], x_recv.at[w, s - 1, j], chip_id(s))
                    copy.start()
                    sends.append(copy)
            else:
                remote(here, here, x_send.at[w, step - 1, j], x_recv.at[w, step - 1, j], y_id).wait_recv()
            copy = remote(here, here, d_send.at[w, step, j], d_recv.at[w, step, j], partner)
            copy.start()
            sends.append(copy)

        for j in range(CHUNKS + 1):
            if j < CHUNKS:
                pass_across(0, j)
            if j > 0:
                for step in range(1, chips):
                    pass_across(step, j - 1)

    def finish(w):
        full = weights[w][1]
        for step in range(chips):
            slot = lax.rem(chip + chips - step, chips) * 2 + 1 - core
            for j in range(CHUNKS):
                here = full.at[rows(1 - dp, slot, j)]
                remote(here, here, d_send.at[w, step, j], d_recv.at[w, step, j], partner).wait_recv()

    relay(0)
    own_q.wait()
    finish(0)
    project(MAXLEN, local, q_out, 0, 0)
    relay(1)
    project(MAXLEN, local, k_out, MAXLEN, 1)
    project(MAXLEN, local, v_out, MAXLEN, 2)
    own_o.wait()
    finish(1)
    out_copy = pltpu.make_async_copy(wo_full, wo_out, local_sem.at[3])
    out_copy.start()
    for j in range(HALO_CHUNKS):
        for side in range(2):
            start = side * (MAXLEN + local) + j * hop

            @pl.when(jnp.logical_not(last if side else first))
            def _():
                (down if side else up)(j).wait_recv()

            norm(start, hop)
            project(start, hop, k_out, start, 1)
            project(start, hop, v_out, start, 2)

    out_copy.wait()

    @pl.when(jnp.logical_not(last))
    def _():
        for j in range(HALO_CHUNKS):
            up(j).wait_send()

    @pl.when(jnp.logical_not(first))
    def _():
        for j in range(HALO_CHUNKS):
            down(j).wait_send()

    for copy in sends:
        copy.wait_send()


def project_all(nx, ny, tok, gain, wq, wo):
    local, width = tok.shape
    long = local + 2 * MAXLEN
    bf16 = jnp.bfloat16
    chips = nx // 2
    anywhere = pl.BlockSpec(memory_space=pl.ANY)
    vmem = pl.BlockSpec(memory_space=pltpu.VMEM)
    dma = pltpu.SemaphoreType.DMA
    shape = jax.ShapeDtypeStruct
    return pl.pallas_call(
        functools.partial(project_kernel, nx, ny),
        out_shape=(
            shape((local, width), bf16), shape((long, width), bf16),
            shape((long, width), bf16), shape((width, width), bf16),
        ),
        in_specs=[anywhere, vmem, anywhere, anywhere],
        out_specs=(vmem, vmem, vmem, anywhere),
        scratch_shapes=[
            pltpu.VMEM((long, width), bf16), pltpu.VMEM((long, width), bf16),
            pltpu.VMEM((width, 3 * width), bf16), pltpu.VMEM((width, width), bf16),
            dma((2, CHUNKS)), dma((2, CHUNKS)),
            dma((2, max(chips - 1, 1), CHUNKS)), dma((2, max(chips - 1, 1), CHUNKS)),
            dma((2, chips, CHUNKS)), dma((2, chips, CHUNKS)),
            dma((2, HALO_CHUNKS)), dma((2, HALO_CHUNKS)), dma((4,)),
        ],
        compiler_params=pltpu.CompilerParams(
            collective_id=0, has_side_effects=True, vmem_limit_bytes=32 * 2**20
        ),
        name="project",
    )(tok, gain, wq, wo)


def head_window(head, size):
    low = head * size // LANES * LANES
    high = -(-(head + 1) * size // LANES) * LANES
    return low, high - low


def attend_kernel(
    lo_ref, nb_ref, begin, end, ids, scale_rows, q, k, v, tok, wo, hidden, pooled,
    context, turned, flat, wide, top, total, acc,
):
    local, width = q.shape
    size = width // HEADS
    long = k.shape[0]
    factor = size ** (-0.5) * 1.4426950408889634

    @pl.loop(0, long // KBLOCK)
    def _(r):
        at = pl.multiple_of(r * KBLOCK, KBLOCK)
        turned[:, pl.ds(at, KBLOCK)] = v[pl.ds(at, KBLOCK)].T

    @pl.loop(0, local // QBLOCK)
    def _(block):
        here = pl.ds(pl.multiple_of(block * QBLOCK, QBLOCK), QBLOCK)
        low = lo_ref[block]
        top[...] = jnp.full(top.shape, FAR, jnp.float32)
        total[...] = jnp.zeros(total.shape, jnp.float32)
        acc[...] = jnp.zeros(acc.shape, jnp.float32)
        q_begin, q_end = begin[:, here], end[:, here]
        flat[...] = q[here].T
        for head in range(HEADS):
            first, span = head_window(head, size)
            row = first + lax.broadcasted_iota(jnp.int32, (span, QBLOCK), 0)
            inside = (row >= head * size) & (row < (head + 1) * size)
            wide[head, :span] = jnp.where(inside, flat[first : first + span], 0).astype(wide.dtype)

        @pl.loop(0, nb_ref[block])
        def _(step):
            wanted = low + step * KBLOCK
            start = pl.multiple_of(jnp.minimum(wanted, long - KBLOCK), LANES)
            there = pl.ds(start, KBLOCK)
            at = start + lax.broadcasted_iota(jnp.int32, (KBLOCK, QBLOCK), 0)
            allowed = (at >= jnp.maximum(q_begin, wanted)) & (at < q_end)
            for head in range(HEADS):
                first, span = head_window(head, size)
                own = pl.ds(head * size, size)
                scores = jnp.dot(
                    k[there, first : first + span], wide[head, :span],
                    preferred_element_type=jnp.float32,
                )
                scores = jnp.where(allowed, scores, FAR)
                old = top[head]
                new = jnp.maximum(old, jnp.max(scores, axis=0, keepdims=True))
                probs = jnp.exp2((scores - new) * factor)
                shrink = jnp.exp2((old - new) * factor)
                total[head] = total[head] * shrink + jnp.sum(probs, axis=0, keepdims=True)
                top[head] = new
                acc[own] = acc[own] * shrink + jnp.dot(
                    turned[own, there], probs.astype(v.dtype), preferred_element_type=jnp.float32
                )

        for head in range(HEADS):
            own = pl.ds(head * size, size)
            flat[own] = (acc[own] / total[head]).astype(flat.dtype)
        context[here] = flat[...].T

    images = pooled.shape[0]
    cols = 256
    labels = lax.broadcasted_iota(jnp.int32, (images, local), 0)
    onehot = jnp.where(labels == ids[...], 1.0, 0.0).astype(jnp.bfloat16)

    @pl.loop(0, width // cols)
    def _(c):
        at = pl.ds(pl.multiple_of(c * cols, cols), cols)
        mixed = jnp.dot(context[...], wo[:, at], preferred_element_type=jnp.float32)
        rounded = (tok[:, at].astype(jnp.float32) + mixed).astype(hidden.dtype)
        hidden[:, at] = rounded
        sums = jnp.dot(onehot, rounded, preferred_element_type=jnp.float32)
        pooled[:, at] = sums / scale_rows[...]


def attend_all(lo, nb, begin, end, ids, counts, q, k, v, tok, wo):
    local, width = tok.shape
    images = counts.shape[0]
    vmem = pl.BlockSpec(memory_space=pltpu.VMEM)
    smem = pl.BlockSpec(memory_space=pltpu.SMEM)
    return pl.pallas_call(
        attend_kernel,
        out_shape=(
            jax.ShapeDtypeStruct((local, width), jnp.bfloat16),
            jax.ShapeDtypeStruct((images, width), jnp.float32),
        ),
        in_specs=[smem, smem] + [vmem] * 9,
        out_specs=(vmem, vmem),
        scratch_shapes=[
            pltpu.VMEM((local, width), jnp.bfloat16),
            pltpu.VMEM((width, k.shape[0]), jnp.bfloat16),
            pltpu.VMEM((width, QBLOCK), jnp.bfloat16),
            pltpu.VMEM((HEADS, 2 * LANES, QBLOCK), jnp.bfloat16),
            pltpu.VMEM((HEADS, 1, QBLOCK), jnp.float32),
            pltpu.VMEM((HEADS, 1, QBLOCK), jnp.float32),
            pltpu.VMEM((width, QBLOCK), jnp.float32),
        ],
        compiler_params=pltpu.CompilerParams(vmem_limit_bytes=26 * 2**20),
        name="attend",
    )(lo, nb, begin, end, ids, counts, q, k, v, tok, wo)


def pool_kernel(nx, ny, parts, out, landed, reduced, send1, recv1, send2, recv2):
    sx, sy, dp = lax.axis_index("sx"), lax.axis_index("sy"), lax.axis_index("dp")
    count = nx * ny
    me = sx * ny + sy

    def device(step):
        peer = lax.rem(me + step, count)
        return peer, (peer // ny, lax.rem(peer, ny), dp)

    barrier = pltpu.get_barrier_semaphore()
    for step in range(1, count):
        pl.semaphore_signal(barrier, inc=1, device_id=device(step)[1], device_id_type=MESH)
    pl.semaphore_wait(barrier, count - 1)
    copies = []
    for step in range(1, count):
        peer, ident = device(step)
        copy = remote(
            parts.at[peer], landed.at[step - 1], send1.at[step - 1], recv1.at[step - 1], ident
        )
        copy.start()
        copies.append(copy)
    value = parts[me].astype(jnp.float32)
    for step in range(1, count):
        copies[step - 1].wait_recv()
        value = value + landed[step - 1].astype(jnp.float32)
    reduced[...] = value.astype(reduced.dtype)
    out[me] = value.astype(out.dtype)
    again = []
    for step in range(1, count):
        copy = remote(reduced, out.at[me], send2.at[step - 1], recv2.at[step - 1], device(step)[1])
        copy.start()
        again.append(copy)
    for step in range(1, count):
        source = lax.rem(me + count - step, count)
        remote(
            reduced, out.at[source], send2.at[step - 1], recv2.at[step - 1], device(step)[1]
        ).wait_recv()
    for copy in copies + again:
        copy.wait_send()


def pool_all(nx, ny, parts):
    count = nx * ny
    images, width = parts.shape
    each = images // count
    grouped = parts.astype(jnp.bfloat16).reshape(count, each, width)
    vmem = pl.BlockSpec(memory_space=pltpu.VMEM)
    dma = pltpu.SemaphoreType.DMA
    out = pl.pallas_call(
        functools.partial(pool_kernel, nx, ny),
        out_shape=jax.ShapeDtypeStruct(grouped.shape, grouped.dtype),
        in_specs=[vmem],
        out_specs=vmem,
        scratch_shapes=[
            pltpu.VMEM((count - 1, each, width), grouped.dtype),
            pltpu.VMEM((each, width), grouped.dtype),
            dma((count - 1,)), dma((count - 1,)), dma((count - 1,)), dma((count - 1,)),
        ],
        compiler_params=pltpu.CompilerParams(collective_id=1, has_side_effects=True),
        name="pool",
    )(grouped)
    return out.reshape(images, width).astype(jnp.float32)


def shards(nx, ny, tokens, lengths, ln_gain, w_qkv, w_out):
    local = tokens.shape[1]
    images = lengths.shape[1]
    tok = tokens[0]
    counts = lengths[0]
    shard = lax.axis_index("sx") * ny + lax.axis_index("sy")
    base = shard * local
    positions = base + jnp.arange(local, dtype=jnp.int32)
    ends = jnp.cumsum(counts)
    offsets = ends - counts
    reached = offsets[None, :] <= positions[:, None]
    ids = jnp.sum(reached.astype(jnp.int32), axis=1) - 1
    shift = base - MAXLEN
    begin = jnp.max(jnp.where(reached, offsets[None, :], 0), axis=1) - shift
    end = jnp.min(jnp.where(ends[None, :] > positions[:, None], ends[None, :], 2**30), axis=1) - shift
    low = begin[::QBLOCK] // LANES * LANES
    high = end[QBLOCK - 1 :: QBLOCK]
    blocks = (high - low + KBLOCK - 1) // KBLOCK
    q, k, v, wo = project_all(nx, ny, tok, ln_gain[None, :], w_qkv, w_out)
    hidden, parts = attend_all(
        low, blocks, begin[None, :], end[None, :], ids[None, :],
        counts.astype(jnp.float32)[:, None], q, k, v, tok, wo,
    )
    pooled = pool_all(nx, ny, parts)
    return (hidden[None], pooled[None])


def solution(mesh):
    in_specs = (P("dp", ("sx", "sy"), None), P("dp", None), P(), P("dp", None), P("dp", None))
    out_specs = (P("dp", ("sx", "sy"), None), P("dp", None, None))
    body = functools.partial(shards, mesh.shape["sx"], mesh.shape["sy"])
    return jax.shard_map(body, mesh=mesh, in_specs=in_specs, out_specs=out_specs, check_vma=False)
```

profile of v0, /device:TPU:0, one launch (start us, length us, event | category | flops | bytes accessed | tf_op | source)
XLA Modules:
  0.0 152.3 jit_solution(8454717467653122491)
XLA Ops:
  0.6 0.7 broadcast_in_dim.35.gain
  1.4 0.7 copy.13
  2.1 0.1 reduce-window.4
  2.2 0.1 reduce
  2.3 0.7 bitcast_convert_fusion
  3.0 0.1 fusion.1
  3.1 0.1 slice.7
  3.2 0.1 slice.6
  3.3 0.1 copy.14.scale_rows
  3.4 0.0 copy-start
  3.4 1.3 copy-done
  4.8 0.0 copy-start.2
  4.8 2.4 %copy-done.2 = bf16[640,3840]{1,0:T(8,128)(2,1)S(1)} copy-done((bf16[640,3840]{1,0:T(8,128)(2,1)S(1)}, bf16[640,3840]{1,0:T(8,128)(2,1)}, u32[]{:S(2)}) %copy-start.2) | copy-done | bytes 4915224
  7.1 0.0 copy-start.3
  7.2 1.4 copy-done.3
  8.6 0.0 copy-start.1
  8.6 87.8 %project.1 = (bf16[512,1280]{1,0:T(8,128)(2,1)S(1)}, bf16[1536,1280]{1,0:T(8,128)(2,1)S(1)}, bf16[1536,1280]{1,0:T(8,128)(2,1)S(1)}, bf16[1280,1280]{1,0:T(8,128)(2,1)S(1)}) custom-call(bf16[512,1280]{1,0:T(8,128)(2,1)S(1)} %bitcast.13, f32[1,1280]{1,0:T(1,128)S(1)} %broadcast_in_dim.35.gain, bf16[640,3840]{1,0:T(8,128)(2,1)S(1)} %copy-done.2, ...), custom_call_target="tpu_custom_call" | custom-call | tf_op jit(solution)/shard_map/project/pallas_call | solution.py:217
  96.4 0.0 copy-done.1
  96.4 30.0 %attend.1 = (bf16[512,1280]{1,0:T(8,128)(2,1)}, f32[64,1280]{1,0:T(8,128)S(1)}) custom-call(s32[2]{0:T(128)S(1)} %get-tuple-element.18.lo_ref, s32[2]{0:T(128)S(1)} %get-tuple-element.17.nb_ref, s32[1,512]{1,0:T(1,128)S(1)} %bitcast.17, s32[1,512]{1,0:T(1,128)S(1)} %bitcast.16, s32[1,512]{1,0:T(1,128)S(1)} %bitcast.15, f32[64,1]{1,0:T(8,128)S(1)} %copy.14.scale_rows, ...), custom_call_target="tpu_custom_call" | custom-call | tf_op jit(solution)/shard_map/attend/pallas_call | solution.py:325
  126.4 0.7 reshape.73.parts
  127.1 23.5 %pool.1 = bf16[16,4,1280]{2,1,0:T(4,128)(2,1)} custom-call(bf16[16,4,1280]{2,1,0:T(4,128)(2,1)} %reshape.73.parts), custom_call_target="tpu_custom_call" | custom-call | tf_op jit(solution)/shard_map/pool/pallas_call | solution.py:395
  150.7 1.7 %reshape.74 = f32[1,64,1280]{2,1,0:T(8,128)} reshape(bf16[16,4,1280]{2,1,0:T(4,128)(2,1)} %pool.1) | data formatting | bytes 491520 | tf_op jit(solution)/shard_map/convert_element_type | solution.py:408
  (5 shorter events, 0.1 us)
Async XLA Ops:
  3.4 1.3 copy-start
  4.8 2.4 %copy-start.2 = (bf16[640,3840]{1,0:T(8,128)(2,1)S(1)}, bf16[640,3840]{1,0:T(8,128)(2,1)}, u32[]{:S(2)}) copy-start(bf16[640,3840]{1,0:T(8,128)(2,1)} %wq.1) | copy-start | bytes 14745604
  7.1 1.4 copy-start.3
  8.6 87.8 %copy-start.1 = (bf16[1,512,1280]{2,1,0:T(8,128)(2,1)S(1)}, bf16[1,512,1280]{2,1,0:T(8,128)(2,1)}, u32[]{:S(2)}) copy-start(bf16[1,512,1280]{2,1,0:T(8,128)(2,1)} %param.5) | copy-start | bytes 3932164
where the time goes:
time: 153 us; the launch traced here: 152 us
  Pallas kernels  141 us (92%)
  local copies, waits for them, and re-layouts  9.25 us (6%)
    pallas_call x1, Pallas kernels, project_all(): pl.pallas_call(functools.partial(project_kernel, nx, ny), out_shape=(shap...  87.8 us
    pallas_call x1, Pallas kernels, attend_all(): pl.pallas_call(attend_kernel, out_shape=(jax.ShapeDtypeStruct((local, wid...  30 us
    pallas_call x1, Pallas kernels, pool_all(): pl.pallas_call(functools.partial(pool_kernel, nx, ny), out_shape=jax.Shap...  23.5 us
    unnamed x8, local copies, waits for them, and re-layouts  5.14 us

commit v1 on v0

v1 whole, which is shorter than its diff:
```python
import functools

import jax
import jax.numpy as jnp
from jax import lax
from jax.experimental import pallas as pl
from jax.experimental.pallas import tpu as pltpu
from jax.sharding import PartitionSpec as P

HEADS = 16
MAXLEN = 512
MESH = pl.DeviceIdType.MESH
GROUPS = 2
WIDE_CHUNKS = 3 * GROUPS
CHUNKS = 4 * GROUPS
HOP = 128
HOPS = MAXLEN // HOP
NEAR = 2
QBLOCK = 256
LANES = 128
ONES = 16
FAR = -1e30


def remote(src, dst, send, recv, device):
    return pltpu.make_async_remote_copy(
        src_ref=src, dst_ref=dst, send_sem=send, recv_sem=recv, device_id=device, device_id_type=MESH
    )


def head_window(head, size):
    low = head * size // LANES * LANES
    high = -(-(head + 1) * size // LANES) * LANES
    return low, high - low


def block_kernel(
    nx, ny, tok, lengths, gain, wq, wo, hidden, pooled,
    toks, normed, wq_full, wo_full, gains, keys, wide, turned, bias, top, acc, flat, context, hid, onehot, parts,
    landed, reduced, gathered,
    y_send, y_recv, x_send, x_recv, d_send, d_recv, h_send, h_recv, s_send, s_recv, g_send, g_recv, local_sem, out_sem,
):
    sx, sy, dp = lax.axis_index("sx"), lax.axis_index("sy"), lax.axis_index("dp")
    chips = nx // 2
    chip, core = sx // 2, lax.rem(sx, 2)
    count = nx * ny
    shard = sx * ny + sy
    first, last = shard == 0, shard == count - 1
    f32, bf16 = jnp.float32, jnp.bfloat16

    local, width = tok.shape
    long = toks.shape[0]
    size = width // HEADS
    half = wq.shape[0]
    quarter = half // nx
    cols = width // GROUPS
    team = HEADS // GROUPS
    images = pooled.shape[0]
    each = images // count
    blocks = local // QBLOCK
    factor = size ** (-0.5) * 1.4426950408889634

    def peer(step):
        other = lax.rem(shard + step, count)
        return other, (other // ny, lax.rem(other, ny), dp)

    prev_id, next_id = peer(count - 1)[1], peer(1)[1]
    y_id = (sx, sy, 1 - dp)
    partner = (chip * 2 + 1 - core, sy, dp)

    def chip_id(step):
        return (lax.rem(chip + step, chips) * 2 + core, sy, dp)

    barrier = pltpu.get_barrier_semaphore()
    for device in [y_id] + [peer(step)[1] for step in range(1, count)]:
        pl.semaphore_signal(barrier, inc=1, device_id=device, device_id_type=MESH)
    own_tokens = pltpu.make_async_copy(tok, toks.at[pl.ds(MAXLEN, local)], local_sem.at[0])
    mine = pl.ds(pl.multiple_of(dp * half, half), half)
    own_q = pltpu.make_async_copy(wq, wq_full.at[mine], local_sem.at[1])
    own_o = pltpu.make_async_copy(wo, wo_full.at[mine], local_sem.at[2])
    own_tokens.start()
    own_q.start()
    own_o.start()
    pl.semaphore_wait(barrier, count)

    def chunk(j):
        if j < WIDE_CHUNKS:
            return wq, wq_full, pl.ds(j % 3 * width + j // 3 * cols, cols)
        return wo, wo_full, pl.ds((j - WIDE_CHUNKS) * cols, cols)

    def rows(owner, slot):
        return pl.ds(pl.multiple_of(owner * half + slot * quarter, quarter), quarter)

    sends = []
    for j in range(CHUNKS):
        part, full, at = chunk(j)
        copy = remote(
            part.at[pl.ds(pl.multiple_of(sx * quarter, quarter), quarter), at],
            full.at[rows(dp, sx), at], y_send.at[j], y_recv.at[j], y_id,
        )
        copy.start()
        sends.append(copy)

    def place(side, hop):
        return MAXLEN + local + hop * HOP if side else MAXLEN - (hop + 1) * HOP

    def up(hop):
        return remote(
            tok.at[pl.ds(local - (hop + 1) * HOP, HOP)], toks.at[pl.ds(place(0, hop), HOP)],
            h_send.at[0, hop], h_recv.at[0, hop], next_id,
        )

    def down(hop):
        return remote(
            tok.at[pl.ds(hop * HOP, HOP)], toks.at[pl.ds(place(1, hop), HOP)],
            h_send.at[1, hop], h_recv.at[1, hop], prev_id,
        )

    @pl.when(jnp.logical_not(last))
    def _():
        for hop in range(HOPS):
            up(hop).start()

    @pl.when(jnp.logical_not(first))
    def _():
        for hop in range(HOPS):
            down(hop).start()

    @pl.when(first)
    def _():
        toks[pl.ds(0, MAXLEN)] = jnp.zeros((MAXLEN, width), toks.dtype)

    @pl.when(last)
    def _():
        toks[pl.ds(MAXLEN + local, MAXLEN)] = jnp.zeros((MAXLEN, width), toks.dtype)

    for i in range(width // LANES):
        gains[:, pl.ds(i * LANES, LANES)] = gain[pl.ds(i, 1), :]

    def norm(start, amount):
        step = 32

        @pl.loop(0, amount // step)
        def _(i):
            where = pl.ds(pl.multiple_of(start + i * step, step), step)
            values = toks[where].astype(f32)
            center = values - jnp.mean(values, axis=-1, keepdims=True)
            spread = jnp.mean(center * center, axis=-1, keepdims=True)
            normed[where] = (center * lax.rsqrt(spread + 1e-05) * gains[...]).astype(bf16)

    def project(start, amount, group, which):
        at = pl.ds(pl.multiple_of(which * width + group * cols, LANES), cols)
        return jnp.dot(normed[pl.ds(start, amount)], wq_full[:, at], preferred_element_type=f32)

    def project_q(start, amount, group):
        columns = (project(start, amount, group, 0) * factor).astype(bf16).T
        at = pl.ds(pl.multiple_of(start - MAXLEN, amount), amount)
        for head in range(team):
            low = head * size - head_window(head, size)[0]
            wide[group * team + head, pl.ds(low, size), at] = columns[head * size : (head + 1) * size]

    def project_k(start, amount, group):
        at = pl.ds(pl.multiple_of(group * cols, LANES), cols)
        keys[pl.ds(start, amount), at] = project(start, amount, group, 1).astype(bf16)

    def project_v(start, amount, group):
        columns = project(start, amount, group, 2).astype(bf16).T
        at = pl.ds(start, amount)
        for head in range(team):
            turned[group * team + head, pl.ds(0, size), at] = columns[head * size : (head + 1) * size]

    def attend(block, group, start, amount, fresh):
        queries = pl.ds(pl.multiple_of(block * QBLOCK, QBLOCK), QBLOCK)
        there = pl.ds(start, amount)
        shade = pl.ds(pl.multiple_of(start - block * QBLOCK, LANES), amount)
        for head in range(team):
            low, span = head_window(head, size)
            slot = group * team + head
            where = block * HEADS + slot
            scores = jnp.dot(
                keys[there, pl.ds(pl.multiple_of(group * cols + low, LANES), span)],
                wide[slot, pl.ds(0, span), queries], preferred_element_type=f32,
            ) + bias[block, shade]
            new = jnp.max(scores, axis=0, keepdims=True)
            if not fresh:
                old = top[where]
                new = jnp.maximum(old, new)
            probs = jnp.exp2(scores - new).astype(bf16)
            mixed = jnp.dot(turned[slot, :, there], probs, preferred_element_type=f32)
            if not fresh:
                mixed = acc[where] * jnp.exp2(old - new) + mixed
            acc[where] = mixed
            top[where] = new

    own_tokens.wait()
    norm(MAXLEN, local)

    wide[...] = jnp.zeros(wide.shape, bf16)
    turned[:, pl.ds(size, ONES), :] = jnp.ones((HEADS, ONES, long), bf16)
    row_lengths = lengths[...].astype(f32)
    to = lax.broadcasted_iota(jnp.int32, (images, images), 0)
    of = lax.broadcasted_iota(jnp.int32, (images, images), 1)
    offsets = jnp.sum(jnp.where(of < to, row_lengths, 0.0), axis=1, keepdims=True)
    amounts = jnp.sum(jnp.where(of == to, row_lengths, 0.0), axis=1, keepdims=True)
    ends = offsets + amounts
    base = shard * local
    spots = (base + lax.broadcasted_iota(jnp.int32, (1, local), 1)).astype(f32)
    inside = (offsets <= spots) & (spots < ends)
    onehot[...] = jnp.where(inside, 1.0, 0.0).astype(bf16)
    begin = jnp.max(jnp.where(inside, offsets, 0.0), axis=0, keepdims=True)
    end = jnp.max(jnp.where(inside, ends, 0.0), axis=0, keepdims=True)
    for block in range(blocks):
        mine_begin = begin[:, block * QBLOCK : (block + 1) * QBLOCK]
        mine_end = end[:, block * QBLOCK : (block + 1) * QBLOCK]
        step = 64

        @pl.loop(0, bias.shape[1] // step)
        def _(i):
            at = pl.multiple_of(i * step, step)
            spot = base - MAXLEN + block * QBLOCK + at + lax.broadcasted_iota(jnp.int32, (step, QBLOCK), 0)
            spot = spot.astype(f32)
            allowed = (spot >= mine_begin) & (spot < mine_end)
            bias[block, pl.ds(at, step)] = jnp.where(allowed, 0.0, FAR)

    def relay_y(j):
        here = chunk(j)[1].at[rows(1 - dp, sx), chunk(j)[2]]
        remote(here, here, y_send.at[j], y_recv.at[j], y_id).wait_recv()
        for step in range(1, chips):
            copy = remote(here, here, x_send.at[step - 1, j], x_recv.at[step - 1, j], chip_id(step))
            copy.start()
            sends.append(copy)
        copy = remote(here, here, d_send.at[0, j], d_recv.at[0, j], partner)
        copy.start()
        sends.append(copy)

    def relay_x(j):
        for step in range(1, chips):
            slot = lax.rem(chip + chips - step, chips) * 2 + core
            here = chunk(j)[1].at[rows(1 - dp, slot), chunk(j)[2]]
            remote(here, here, x_send.at[step - 1, j], x_recv.at[step - 1, j], y_id).wait_recv()
            copy = remote(here, here, d_send.at[step, j], d_recv.at[step, j], partner)
            copy.start()
            sends.append(copy)

    def complete(j):
        for step in range(chips):
            slot = lax.rem(chip + chips - step, chips) * 2 + 1 - core
            here = chunk(j)[1].at[rows(1 - dp, slot), chunk(j)[2]]
            remote(here, here, d_send.at[step, j], d_recv.at[step, j], partner).wait_recv()

    def own_chunk(j):
        group, which = j // 3, j % 3
        complete(j)

        @pl.loop(0, blocks)
        def _(i):
            start = pl.multiple_of(MAXLEN + i * QBLOCK, QBLOCK)
            (project_q, project_k, project_v)[which](start, QBLOCK, group)

        if which == 2:

            @pl.loop(0, blocks)
            def _(block):
                attend(block, group, MAXLEN, local, True)

    own_q.wait()
    for j in range(CHUNKS):
        relay_y(j)
        if j >= 1:
            relay_x(j - 1)
        if j >= 2:
            own_chunk(j - 2)

    def arrived(hop):
        for side in range(2):

            @pl.when(jnp.logical_not(last if side else first))
            def _():
                (down if side else up)(hop).wait_recv()

            norm(place(side, hop), HOP)

    for hop in range(NEAR):
        arrived(hop)
    near = NEAR * HOP

    @pl.loop(0, 2)
    def _(side):
        start = pl.multiple_of(MAXLEN - near + side * (local + near), near)

        @pl.loop(0, GROUPS)
        def _(group):
            project_k(start, near, group)
            project_v(start, near, group)

            @pl.loop(0, blocks)
            def _(block):
                attend(block, group, start, near, False)

    relay_x(CHUNKS - 1)
    for hop in range(NEAR, HOPS):
        arrived(hop)

        @pl.loop(0, 2)
        def _(side):
            start = pl.multiple_of(place(0, hop) + side * (place(1, hop) - place(0, hop)), HOP)

            @pl.loop(0, GROUPS)
            def _(group):
                project_k(start, HOP, group)
                project_v(start, HOP, group)
                attend(side * (blocks - 1), group, start, HOP, False)

    @pl.loop(0, blocks)
    def _(block):
        @pl.loop(0, GROUPS)
        def _(group):
            for head in range(team):
                where = block * HEADS + group * team + head
                share = 1.0 / acc[where, pl.ds(size, 1)]
                at = pl.ds(pl.multiple_of(group * cols + head * size, size), size)
                flat[at] = (acc[where, pl.ds(0, size)] * share).astype(bf16)

        context[pl.ds(pl.multiple_of(block * QBLOCK, QBLOCK), QBLOCK)] = flat[...].T

    own_o.wait()
    for j in range(WIDE_CHUNKS, CHUNKS):
        complete(j)
    tile = 256

    def put(c):
        at = pl.ds(pl.multiple_of(c * tile, tile), tile)
        return pltpu.make_async_copy(hid.at[:, at], hidden.at[:, at], out_sem.at[c])

    @pl.loop(0, width // tile)
    def _(c):
        at = pl.ds(pl.multiple_of(c * tile, tile), tile)
        mixed = jnp.dot(context[...], wo_full[:, at], preferred_element_type=f32)
        rounded = (toks[pl.ds(MAXLEN, local), at].astype(f32) + mixed).astype(bf16)
        hid[:, at] = rounded
        put(c).start()
        means = jnp.dot(onehot[...], rounded, preferred_element_type=f32) / amounts
        for p in range(count):
            parts[p, :, at] = means[p * each : (p + 1) * each].astype(bf16)

    copies = []
    for step in range(1, count):
        other, ident = peer(step)
        copy = remote(parts.at[other], landed.at[step - 1], s_send.at[step - 1], s_recv.at[step - 1], ident)
        copy.start()
        copies.append(copy)
    value = parts[shard].astype(f32)
    for step in range(1, count):
        copies[step - 1].wait_recv()
        value = value + landed[step - 1].astype(f32)
    reduced[...] = value.astype(bf16)
    gathered[shard] = value.astype(bf16)
    for step in range(1, count):
        copy = remote(reduced, gathered.at[shard], g_send.at[step - 1], g_recv.at[step - 1], peer(step)[1])
        copy.start()
        copies.append(copy)
    for step in range(1, count):
        source = peer(count - step)[0]
        remote(
            reduced, gathered.at[source], g_send.at[step - 1], g_recv.at[step - 1], peer(step)[1]
        ).wait_recv()
    for p in range(count):
        pooled[p * each : (p + 1) * each] = gathered[p].astype(f32)

    @pl.loop(0, width // tile)
    def _(c):
        put(c).wait()

    @pl.when(jnp.logical_not(last))
    def _():
        for hop in range(HOPS):
            up(hop).wait_send()

    @pl.when(jnp.logical_not(first))
    def _():
        for hop in range(HOPS):
            down(hop).wait_send()

    for copy in sends + copies:
        copy.wait_send()


def shards(nx, ny, tokens, lengths, ln_gain, w_qkv, w_out):
    local, width = tokens.shape[1:]
    images = lengths.shape[1]
    count = nx * ny
    chips = nx // 2
    each = images // count
    size = width // HEADS
    long = local + 2 * MAXLEN
    blocks = local // QBLOCK
    f32, bf16 = jnp.float32, jnp.bfloat16
    anywhere = pl.BlockSpec(memory_space=pl.ANY)
    vmem = pl.BlockSpec(memory_space=pltpu.VMEM)
    dma = pltpu.SemaphoreType.DMA
    hidden, pooled = pl.pallas_call(
        functools.partial(block_kernel, nx, ny),
        out_shape=(
            jax.ShapeDtypeStruct((local, width), bf16), jax.ShapeDtypeStruct((images, width), f32),
        ),
        in_specs=[anywhere, vmem, vmem, anywhere, anywhere],
        out_specs=(anywhere, vmem),
        scratch_shapes=[
            pltpu.VMEM((long, width), bf16), pltpu.VMEM((long, width), bf16),
            pltpu.VMEM((width, 3 * width), bf16), pltpu.VMEM((width, width), bf16),
            pltpu.VMEM((1, width), f32),
            pltpu.VMEM((long, width), bf16),
            pltpu.VMEM((HEADS, 2 * LANES, local), bf16),
            pltpu.VMEM((HEADS, size + ONES, long), bf16),
            pltpu.VMEM((blocks, QBLOCK + 2 * MAXLEN, QBLOCK), f32),
            pltpu.VMEM((blocks * HEADS, 1, QBLOCK), f32),
            pltpu.VMEM((blocks * HEADS, size + ONES, QBLOCK), f32),
            pltpu.VMEM((width, QBLOCK), bf16),
            pltpu.VMEM((local, width), bf16), pltpu.VMEM((local, width), bf16),
            pltpu.VMEM((images, local), bf16),
            pltpu.VMEM((count, each, width), bf16), pltpu.VMEM((count - 1, each, width), bf16),
            pltpu.VMEM((each, width), bf16), pltpu.VMEM((count, each, width), bf16),
            dma((CHUNKS,)), dma((CHUNKS,)),
            dma((max(chips - 1, 1), CHUNKS)), dma((max(chips - 1, 1), CHUNKS)),
            dma((chips, CHUNKS)), dma((chips, CHUNKS)),
            dma((2, HOPS)), dma((2, HOPS)),
            dma((count - 1,)), dma((count - 1,)), dma((count - 1,)), dma((count - 1,)),
            dma((3,)), dma((width // 256,)),
        ],
        compiler_params=pltpu.CompilerParams(
            collective_id=0, has_side_effects=True, vmem_limit_bytes=60 * 2**20
        ),
        name="block",
    )(tokens[0], lengths, ln_gain.reshape(width // LANES, LANES), w_qkv, w_out)
    return (hidden[None], pooled[None])


def solution(mesh):
    in_specs = (P("dp", ("sx", "sy"), None), P("dp", None), P(), P("dp", None), P("dp", None))
    out_specs = (P("dp", ("sx", "sy"), None), P("dp", None, None))
    body = functools.partial(shards, mesh.shape["sx"], mesh.shape["sy"])
    return jax.shard_map(body, mesh=mesh, in_specs=in_specs, out_specs=out_specs, check_vma=False)
```

time: 153 us -> 136 us (0.89)
  Pallas kernels: 141 us -> 132 us
  local copies, waits for them, and re-layouts: 9.25 us -> 3.23 us
    pallas_call x3 -> x1, Pallas kernels: 141 us -> 132 us  [shards(): pl.pallas_call(functools.partial(block_kernel, nx, ny), out_shape=(jax.Sh...]
    unnamed x8 -> x4, local copies, waits for them, and re-layouts: 5.14 us -> 3.23 us
    convert_element_type x2 -> x0, local copies, waits for them, and re-layouts: 1.76 us -> none  [the longest x1 1.66 us: pool_all(): return out.reshape(images, width).astype(jnp.float32)]
where the time goes in v1:
time: 136 us
  Pallas kernels  132 us (97%)
  local copies, waits for them, and re-layouts  3.23 us (2%)
    pallas_call x1, Pallas kernels, shards(): pl.pallas_call(functools.partial(block_kernel, nx, ny), out_shape=(jax.Sh...  132 us
    unnamed x4, local copies, waits for them, and re-layouts  3.23 us

profile of v1, /device:TPU:0, one launch (start us, length us, event | category | flops | bytes accessed | tf_op | source)
XLA Modules:
  0.0 135.8 jit_solution(4041652654772123956)
XLA Ops:
  0.6 131.9 %block.1 = (bf16[512,1280]{1,0:T(8,128)(2,1)}, f32[64,1280]{1,0:T(8,128)}) custom-call(bf16[512,1280]{1,0:T(8,128)(2,1)} %bitcast.4, s32[1,64]{1,0:T(1,128)} %lengths.1, f32[10,128]{1,0:T(8,128)} %bitcast.7, bf16[640,3840]{1,0:T(8,128)(2,1)} %wq.1, bf16[640,1280]{1,0:T(8,128)(2,1)} %wo.1), custom_call_target="tpu_custom_call" | custom-call | tf_op jit(solution)/shard_map/block/pallas_call | solution.py:401
  132.5 0.0 copy-start
  132.6 2.5 %copy.9 = bf16[1,512,1280]{2,1,0:T(8,128)(2,1)} copy(bf16[1,512,1280]{2,1,0:T(8,128)(2,1)} %bitcast.5) | data formatting | bytes 2621440
  135.1 0.0 copy-done
  135.1 0.7 copy.10
Async XLA Ops:
  132.5 2.5 %copy-start = (f32[64,1280]{1,0:T(8,128)S(1)}, f32[64,1280]{1,0:T(8,128)}, u32[]{:S(2)}) copy-start(f32[64,1280]{1,0:T(8,128)} %get-tuple-element.5) | copy-start | bytes 983044

commit v2 on v1

v2 whole, which is shorter than its diff:
```python
import functools

import jax
import jax.numpy as jnp
from jax import lax
from jax.experimental import pallas as pl
from jax.experimental.pallas import tpu as pltpu
from jax.sharding import PartitionSpec as P

HEADS = 16
MAXLEN = 512
MESH = pl.DeviceIdType.MESH
GROUPS = 2
WIDE_CHUNKS = 3 * GROUPS
CHUNKS = 4 * GROUPS
HOP = 128
HOPS = MAXLEN // HOP
NEAR = 2
QBLOCK = 256
LANES = 128
ONES = 16
FAR = -1e30


def remote(src, dst, send, recv, device):
    return pltpu.make_async_remote_copy(
        src_ref=src, dst_ref=dst, send_sem=send, recv_sem=recv, device_id=device, device_id_type=MESH
    )


def head_window(head, size):
    low = head * size // LANES * LANES
    high = -(-(head + 1) * size // LANES) * LANES
    return low, high - low


def block_kernel(
    nx, ny, tok, lengths_in, gain_in, wq, wo, hidden, pooled,
    lengths, gain, toks, normed, wq_full, wo_full, gains, keys, wide, turned, bias, top, acc, scores, probs, flat, context, onehot, sums, parts,
    landed, reduced, gathered,
    y_send, y_recv, x_send, x_recv, d_send, d_recv, h_send, h_recv, s_send, s_recv, g_send, g_recv, local_sem,
):
    sx, sy, dp = lax.axis_index("sx"), lax.axis_index("sy"), lax.axis_index("dp")
    chips = nx // 2
    chip, core = sx // 2, lax.rem(sx, 2)
    count = nx * ny
    shard = sx * ny + sy
    first, last = shard == 0, shard == count - 1
    f32, bf16 = jnp.float32, jnp.bfloat16

    local, width = tok.shape
    long = toks.shape[0]
    size = width // HEADS
    half = wq.shape[0]
    quarter = half // nx
    cols = width // GROUPS
    team = HEADS // GROUPS
    images = pooled.shape[0]
    each = images // count
    blocks = local // QBLOCK
    factor = size ** (-0.5) * 1.4426950408889634

    def peer(step):
        other = lax.rem(shard + step, count)
        return other, (other // ny, lax.rem(other, ny), dp)

    prev_id, next_id = peer(count - 1)[1], peer(1)[1]
    y_id = (sx, sy, 1 - dp)
    partner = (chip * 2 + 1 - core, sy, dp)

    def chip_id(step):
        return (lax.rem(chip + step, chips) * 2 + core, sy, dp)

    barrier = pltpu.get_barrier_semaphore()
    for device in [y_id] + [peer(step)[1] for step in range(1, count)]:
        pl.semaphore_signal(barrier, inc=1, device_id=device, device_id_type=MESH)
    own_tokens = pltpu.make_async_copy(tok, toks.at[pl.ds(MAXLEN, local)], local_sem.at[0])
    mine = pl.ds(pl.multiple_of(dp * half, half), half)

    def chunk(j):
        if j < WIDE_CHUNKS:
            return wq, pl.ds((j + 1) % 3 * width + j // 3 * cols, cols), wq_full, pl.ds(j * cols, cols)
        at = pl.ds((j - WIDE_CHUNKS) * cols, cols)
        return wo, at, wo_full, at

    own_weights = []
    for j in range(CHUNKS):
        part, at, full, to = chunk(j)
        own_weights.append(pltpu.make_async_copy(part.at[:, at], full.at[mine, to], local_sem.at[1 + j]))
    small = (
        pltpu.make_async_copy(lengths_in, lengths, local_sem.at[1 + CHUNKS]),
        pltpu.make_async_copy(gain_in, gain, local_sem.at[2 + CHUNKS]),
    )
    for copy in small:
        copy.start()
    own_tokens.start()
    for copy in own_weights:
        copy.start()
    pl.semaphore_wait(barrier, count)

    def rows(owner, slot):
        return pl.ds(pl.multiple_of(owner * half + slot * quarter, quarter), quarter)

    sends = []
    for j in range(CHUNKS):
        part, at, full, to = chunk(j)
        copy = remote(
            part.at[pl.ds(pl.multiple_of(sx * quarter, quarter), quarter), at],
            full.at[rows(dp, sx), to], y_send.at[j], y_recv.at[j], y_id,
        )
        copy.start()
        sends.append(copy)

    def place(side, hop):
        return MAXLEN + local + hop * HOP if side else MAXLEN - (hop + 1) * HOP

    def up(hop):
        return remote(
            tok.at[pl.ds(local - (hop + 1) * HOP, HOP)], toks.at[pl.ds(place(0, hop), HOP)],
            h_send.at[0, hop], h_recv.at[0, hop], next_id,
        )

    def down(hop):
        return remote(
            tok.at[pl.ds(hop * HOP, HOP)], toks.at[pl.ds(place(1, hop), HOP)],
            h_send.at[1, hop], h_recv.at[1, hop], prev_id,
        )

    for hop in range(HOPS):
        for side in range(2):

            @pl.when(jnp.logical_not(first if side else last))
            def _():
                (down if side else up)(hop).start()

    @pl.when(first)
    def _():
        toks[pl.ds(0, MAXLEN)] = jnp.zeros((MAXLEN, width), toks.dtype)

    @pl.when(last)
    def _():
        toks[pl.ds(MAXLEN + local, MAXLEN)] = jnp.zeros((MAXLEN, width), toks.dtype)

    for copy in small:
        copy.wait()
    for i in range(width // LANES):
        gains[:, pl.ds(i * LANES, LANES)] = gain[pl.ds(i, 1), :]

    def norm(start, amount):
        step = HOP

        @pl.loop(0, amount // step)
        def _(i):
            where = pl.ds(pl.multiple_of(start + i * step, step), step)
            values = toks[where].astype(f32)
            center = values - jnp.mean(values, axis=-1, keepdims=True)
            spread = jnp.mean(center * center, axis=-1, keepdims=True)
            normed[where] = (center * lax.rsqrt(spread + 1e-05) * gains[...]).astype(bf16)

    def project(start, amount, group, which, parts_of):
        at = pl.ds(pl.multiple_of((group * 3 + which) * cols, LANES), parts_of * cols)
        return jnp.dot(normed[pl.ds(start, amount)], wq_full[:, at], preferred_element_type=f32)

    def project_q(start, amount, group):
        columns = (project(start, amount, group, 2, 1) * factor).astype(bf16).T
        at = pl.ds(pl.multiple_of(start - MAXLEN, amount), amount)
        for head in range(team):
            low = head * size - head_window(head, size)[0]
            wide[group * team + head, pl.ds(low, size), at] = columns[head * size : (head + 1) * size]

    def project_kv(start, amount, group):
        both = project(start, amount, group, 0, 2).astype(bf16)
        here = pl.ds(start, amount)
        keys[here, pl.ds(pl.multiple_of(group * cols, LANES), cols)] = both[:, :cols]
        columns = both[:, cols:].T
        for head in range(team):
            turned[group * team + head, pl.ds(0, size), here] = columns[head * size : (head + 1) * size]

    def attend(block, group, start, amount, fresh, lane=0, lanes=QBLOCK):
        queries = pl.ds(pl.multiple_of(block * QBLOCK + lane, LANES), lanes)
        within = pl.ds(lane, lanes)
        there = pl.ds(start, amount)
        shade = pl.ds(pl.multiple_of(start - block * QBLOCK, LANES), amount)
        some = (pl.ds(0, amount), pl.ds(0, lanes))
        tops, shrinks = [], []
        for head in range(team):
            low, span = head_window(head, size)
            slot = group * team + head
            found = jnp.dot(
                keys[there, pl.ds(pl.multiple_of(group * cols + low, LANES), span)],
                wide[slot, pl.ds(0, span), queries], preferred_element_type=f32,
            ) + bias[block, shade, within]
            scores[(head,) + some] = found
            tops.append(jnp.max(found, axis=0, keepdims=True))
        for head in range(team):
            where = block * HEADS + group * team + head
            new = tops[head]
            if not fresh:
                old = top[where, :, within]
                new = jnp.maximum(old, new)
                shrinks.append(jnp.exp2(old - new))
            top[where, :, within] = new
            probs[(head,) + some] = jnp.exp2(scores[(head,) + some] - new).astype(bf16)
        for head in range(team):
            slot = group * team + head
            where = block * HEADS + slot
            mixed = jnp.dot(turned[slot, :, there], probs[(head,) + some], preferred_element_type=f32)
            if not fresh:
                mixed = acc[where, :, within] * shrinks[head] + mixed
            acc[where, :, within] = mixed

    own_tokens.wait()
    norm(MAXLEN, local)

    wide[...] = jnp.zeros(wide.shape, bf16)
    turned[:, pl.ds(size, ONES), :] = jnp.ones((HEADS, ONES, long), bf16)
    row_lengths = lengths[...].astype(f32)
    to = lax.broadcasted_iota(jnp.int32, (images, images), 0)
    of = lax.broadcasted_iota(jnp.int32, (images, images), 1)
    offsets = jnp.sum(jnp.where(of < to, row_lengths, 0.0), axis=1, keepdims=True)
    amounts = jnp.sum(jnp.where(of == to, row_lengths, 0.0), axis=1, keepdims=True)
    ends = offsets + amounts
    base = shard * local
    spots = (base + lax.broadcasted_iota(jnp.int32, (1, local), 1)).astype(f32)
    inside = (offsets <= spots) & (spots < ends)
    onehot[...] = jnp.where(inside, 1.0, 0.0).astype(bf16)
    begin = jnp.max(jnp.where(inside, offsets, 0.0), axis=0, keepdims=True)
    end = jnp.max(jnp.where(inside, ends, 0.0), axis=0, keepdims=True)
    for block in range(blocks):
        mine_begin = begin[:, block * QBLOCK : (block + 1) * QBLOCK]
        mine_end = end[:, block * QBLOCK : (block + 1) * QBLOCK]
        step = 64

        @pl.loop(0, bias.shape[1] // step)
        def _(i):
            at = pl.multiple_of(i * step, step)
            spot = base - MAXLEN + block * QBLOCK + at + lax.broadcasted_iota(jnp.int32, (step, QBLOCK), 0)
            spot = spot.astype(f32)
            allowed = (spot >= mine_begin) & (spot < mine_end)
            bias[block, pl.ds(at, step)] = jnp.where(allowed, 0.0, FAR)

    def relay_y(j):
        here = chunk(j)[2].at[rows(1 - dp, sx), chunk(j)[3]]
        remote(here, here, y_send.at[j], y_recv.at[j], y_id).wait_recv()
        for step in range(1, chips):
            copy = remote(here, here, x_send.at[step - 1, j], x_recv.at[step - 1, j], chip_id(step))
            copy.start()
            sends.append(copy)
        copy = remote(here, here, d_send.at[0, j], d_recv.at[0, j], partner)
        copy.start()
        sends.append(copy)

    def relay_x(j):
        for step in range(1, chips):
            slot = lax.rem(chip + chips - step, chips) * 2 + core
            here = chunk(j)[2].at[rows(1 - dp, slot), chunk(j)[3]]
            remote(here, here, x_send.at[step - 1, j], x_recv.at[step - 1, j], y_id).wait_recv()
            copy = remote(here, here, d_send.at[step, j], d_recv.at[step, j], partner)
            copy.start()
            sends.append(copy)

    def complete(j):
        for step in range(chips):
            slot = lax.rem(chip + chips - step, chips) * 2 + 1 - core
            here = chunk(j)[2].at[rows(1 - dp, slot), chunk(j)[3]]
            remote(here, here, d_send.at[step, j], d_recv.at[step, j], partner).wait_recv()

    def arrived(hop):
        for side in range(2):

            @pl.when(jnp.logical_not(last if side else first))
            def _():
                (down if side else up)(hop).wait_recv()

            norm(place(side, hop), HOP)

    near = NEAR * HOP

    near_starts = (MAXLEN - near, MAXLEN + local)

    def near_kv(group):
        for side in range(2):
            project_kv(near_starts[side], near, group)

    def near_attend(group):
        @pl.loop(0, 2)
        def _(side):
            start = pl.multiple_of(near_starts[0] + side * (near_starts[1] - near_starts[0]), near)

            @pl.loop(0, blocks)
            def _(block):
                attend(block, group, start, near, False)

    def own_attend(group):
        @pl.loop(0, blocks)
        def _(block):
            attend(block, group, MAXLEN, local, True)

    def ready(*chunks):
        for j in chunks:
            complete(j)
            own_weights[j].wait()

    def far(hop):
        arrived(hop)

        @pl.loop(0, GROUPS)
        def _(group):
            for side in range(2):
                project_kv(place(side, hop), HOP, group)
            for side in range(2):
                lanes = min(QBLOCK, (HOPS - hop) * HOP)
                attend(side * (blocks - 1), group, place(side, hop), HOP, False, side * (QBLOCK - lanes), lanes)

    tile = 256

    def finish(start, amount):
        for at in range(start, start + amount, HOP):
            block, lane = at // QBLOCK, at % QBLOCK

            @pl.loop(0, GROUPS)
            def _(group):
                for head in range(team):
                    where = block * HEADS + group * team + head
                    share = 1.0 / acc[where, pl.ds(size, 1), pl.ds(lane, HOP)]
                    rows_at = pl.ds(pl.multiple_of(group * cols + head * size, size), size)
                    flat[rows_at] = (acc[where, pl.ds(0, size), pl.ds(lane, HOP)] * share).astype(bf16)

            context[pl.ds(at, HOP)] = flat[...].T

    def emit(start, amount):
        where = pl.ds(start, amount)

        @pl.loop(0, width // tile)
        def _(c):
            at = pl.ds(pl.multiple_of(c * tile, tile), tile)
            mixed = jnp.dot(context[where], wo_full[:, at], preferred_element_type=f32)
            hidden[where, at] = (toks[pl.ds(MAXLEN + start, amount), at].astype(f32) + mixed).astype(bf16)

    def relay(j):
        relay_y(j)
        if j:
            relay_x(j - 1)

    for j in range(4):
        relay(j)
    ready(0, 1)
    project_kv(MAXLEN, local, 0)
    ready(2)
    project_q(MAXLEN, local, 0)
    relay(4)
    own_attend(0)
    relay(5)
    arrived(0)
    relay_x(5)
    arrived(1)
    near_kv(0)
    ready(3, 4)
    project_kv(MAXLEN, local, 1)
    relay_y(6)
    near_attend(0)
    ready(5)
    project_q(MAXLEN, local, 1)
    relay_x(6)
    relay_y(7)
    own_attend(1)
    near_kv(1)
    relay_x(7)
    near_attend(1)
    for hop in range(NEAR, HOPS - 1):
        far(hop)
    ready(*range(WIDE_CHUNKS, CHUNKS))
    finish(HOP, local - 2 * HOP)
    emit(HOP, local - 2 * HOP)
    far(HOPS - 1)
    for start in (0, local - HOP):
        finish(start, HOP)
    for start in (0, local - HOP):
        emit(start, HOP)

    sums[...] = jnp.dot(onehot[...], hidden[...], preferred_element_type=f32) / amounts
    for p in range(count):
        parts[p] = sums[p * each : (p + 1) * each].astype(bf16)

    copies = []
    for step in range(1, count):
        other, ident = peer(step)
        copy = remote(parts.at[other], landed.at[step - 1], s_send.at[step - 1], s_recv.at[step - 1], ident)
        copy.start()
        copies.append(copy)
    value = parts[shard].astype(f32)
    for step in range(1, count):
        copies[step - 1].wait_recv()
        value = value + landed[step - 1].astype(f32)
    reduced[...] = value.astype(bf16)
    gathered[shard] = value.astype(bf16)
    for step in range(1, count):
        copy = remote(reduced, gathered.at[shard], g_send.at[step - 1], g_recv.at[step - 1], peer(step)[1])
        copy.start()
        copies.append(copy)
    for step in range(1, count):
        source = peer(count - step)[0]
        remote(
            reduced, gathered.at[source], g_send.at[step - 1], g_recv.at[step - 1], peer(step)[1]
        ).wait_recv()
    for p in range(count):
        pooled[p * each : (p + 1) * each] = gathered[p].astype(f32)


    for side in range(2):

        @pl.when(jnp.logical_not(first if side else last))
        def _():
            for hop in range(HOPS):
                (down if side else up)(hop).wait_send()

    for copy in sends + copies:
        copy.wait_send()


def shards(nx, ny, tokens, lengths, ln_gain, w_qkv, w_out):
    local, width = tokens.shape[1:]
    images = lengths.shape[1]
    count = nx * ny
    chips = nx // 2
    each = images // count
    size = width // HEADS
    long = local + 2 * MAXLEN
    blocks = local // QBLOCK
    team = HEADS // GROUPS
    f32, bf16 = jnp.float32, jnp.bfloat16
    hbm = pl.BlockSpec(memory_space=pltpu.HBM)
    vmem = pl.BlockSpec(memory_space=pltpu.VMEM)
    dma = pltpu.SemaphoreType.DMA
    hidden, pooled = pl.pallas_call(
        functools.partial(block_kernel, nx, ny),
        out_shape=(
            jax.ShapeDtypeStruct((local, width), bf16), jax.ShapeDtypeStruct((images, width), f32),
        ),
        in_specs=[hbm] * 5,
        out_specs=(vmem, vmem),
        scratch_shapes=[
            pltpu.VMEM((1, images), jnp.int32), pltpu.VMEM((width // LANES, LANES), f32),
            pltpu.VMEM((long, width), bf16), pltpu.VMEM((long, width), bf16),
            pltpu.VMEM((width, 3 * width), bf16), pltpu.VMEM((width, width), bf16),
            pltpu.VMEM((1, width), f32),
            pltpu.VMEM((long, width), bf16),
            pltpu.VMEM((HEADS, 2 * LANES, local), bf16),
            pltpu.VMEM((HEADS, size + ONES, long), bf16),
            pltpu.VMEM((blocks, QBLOCK + 2 * MAXLEN, QBLOCK), f32),
            pltpu.VMEM((blocks * HEADS, 1, QBLOCK), f32),
            pltpu.VMEM((blocks * HEADS, size + ONES, QBLOCK), f32),
            pltpu.VMEM((team, local, QBLOCK), f32), pltpu.VMEM((team, local, QBLOCK), bf16),
            pltpu.VMEM((width, HOP), bf16),
            pltpu.VMEM((local, width), bf16),
            pltpu.VMEM((images, local), bf16), pltpu.VMEM((images, width), f32),
            pltpu.VMEM((count, each, width), bf16), pltpu.VMEM((count - 1, each, width), bf16),
            pltpu.VMEM((each, width), bf16), pltpu.VMEM((count, each, width), bf16),
            dma((CHUNKS,)), dma((CHUNKS,)),
            dma((max(chips - 1, 1), CHUNKS)), dma((max(chips - 1, 1), CHUNKS)),
            dma((chips, CHUNKS)), dma((chips, CHUNKS)),
            dma((2, HOPS)), dma((2, HOPS)),
            dma((count - 1,)), dma((count - 1,)), dma((count - 1,)), dma((count - 1,)),
            dma((3 + CHUNKS,)),
        ],
        compiler_params=pltpu.CompilerParams(
            collective_id=0, has_side_effects=True, vmem_limit_bytes=51 * 2**20 + count * 2**16
        ),
        name="block",
    )(tokens[0], lengths, ln_gain.reshape(width // LANES, LANES), w_qkv, w_out)
    return (hidden[None], pooled[None])


def solution(mesh):
    in_specs = (P("dp", ("sx", "sy"), None), P("dp", None), P(), P("dp", None), P("dp", None))
    out_specs = (P("dp", ("sx", "sy"), None), P("dp", None, None))
    body = functools.partial(shards, mesh.shape["sx"], mesh.shape["sy"])
    return jax.shard_map(body, mesh=mesh, in_specs=in_specs, out_specs=out_specs, check_vma=False)
```

time: 136 us -> 96.5 us (0.71)
  Pallas kernels: 132 us -> 92.5 us
    pallas_call x1, Pallas kernels: 132 us -> 92.5 us  [shards(): pl.pallas_call(functools.partial(block_kernel, nx, ny), out_shape=(jax.Sh...]
    unnamed x4 -> x6, local copies, waits for them, and re-layouts: 3.23 us -> 3.13 us
where the time goes in v2:
time: 96.5 us; the launch traced here: 96.3 us
  Pallas kernels  92.5 us (96%)
  local copies, waits for them, and re-layouts  3.13 us (3%)
    pallas_call x1, Pallas kernels, shards(): pl.pallas_call(functools.partial(block_kernel, nx, ny), out_shape=(jax.Sh...  92.5 us
    unnamed x6, local copies, waits for them, and re-layouts  3.13 us

profile of v2, /device:TPU:0, one launch (start us, length us, event | category | flops | bytes accessed | tf_op | source)
XLA Modules:
  0.0 96.3 jit_solution(10543910663773987594)
XLA Ops:
  0.6 0.0 copy-start
  0.6 0.7 copy-done
  1.3 0.0 copy-start.1
  1.3 0.7 copy-done.1
  2.0 92.5 %block.1 = (bf16[512,1280]{1,0:T(8,128)(2,1)S(1)}, f32[64,1280]{1,0:T(8,128)S(1)}) custom-call(bf16[512,1280]{1,0:T(8,128)(2,1)} %bitcast.7, s32[1,64]{1,0:T(1,128)S(1)} %copy-done.1, f32[10,128]{1,0:T(8,128)S(1)} %bitcast.6, bf16[640,3840]{1,0:T(8,128)(2,1)} %wq.1, bf16[640,1280]{1,0:T(8,128)(2,1)} %wo.1), custom_call_target="tpu_custom_call" | custom-call | tf_op jit(solution)/shard_map/block/pallas_call | solution.py:435
  94.5 1.1 %copy.9 = bf16[1,512,1280]{2,1,0:T(8,128)(2,1)} copy(bf16[1,512,1280]{2,1,0:T(8,128)(2,1)S(1)} %bitcast.4) | data formatting | bytes 2621440
  95.6 0.7 copy.10
Async XLA Ops:
  0.6 0.7 copy-start
  1.3 0.7 copy-start.1

commit v3 on v2

--- a/solution.py
+++ b/solution.py
@@ -146,7 +146,7 @@
     for i in range(width // LANES):
         gains[:, pl.ds(i * LANES, LANES)] = gain[pl.ds(i, 1), :]
 
-    def norm(start, amount):
+    def norm(start, amount, to):
         step = HOP
 
         @pl.loop(0, amount // step)
@@ -155,7 +155,7 @@
             values = toks[where].astype(f32)
             center = values - jnp.mean(values, axis=-1, keepdims=True)
             spread = jnp.mean(center * center, axis=-1, keepdims=True)
-            normed[where] = (center * lax.rsqrt(spread + 1e-05) * gains[...]).astype(bf16)
+            normed[pl.ds(pl.multiple_of(to + i * step, step), step)] = (center * lax.rsqrt(spread + 1e-05) * gains[...]).astype(bf16)
 
     def project(start, amount, group, which, parts_of):
         at = pl.ds(pl.multiple_of((group * 3 + which) * cols, LANES), parts_of * cols)
@@ -168,30 +168,39 @@
             low = head * size - head_window(head, size)[0]
             wide[group * team + head, pl.ds(low, size), at] = columns[head * size : (head + 1) * size]
 
-    def project_kv(start, amount, group):
+    def project_kv(start, amount, group, places=None):
         both = project(start, amount, group, 0, 2).astype(bf16)
-        here = pl.ds(start, amount)
-        keys[here, pl.ds(pl.multiple_of(group * cols, LANES), cols)] = both[:, :cols]
         columns = both[:, cols:].T
-        for head in range(team):
-            turned[group * team + head, pl.ds(0, size), here] = columns[head * size : (head + 1) * size]
-
-    def attend(block, group, start, amount, fresh, lane=0, lanes=QBLOCK):
+        places = places or (start,)
+        each_part = amount // len(places)
+        for i, to in enumerate(places):
+            part = slice(i * each_part, (i + 1) * each_part)
+            here = pl.ds(to, each_part)
+            keys[here, pl.ds(pl.multiple_of(group * cols, LANES), cols)] = both[part, :cols]
+            for head in range(team):
+                turned[group * team + head, pl.ds(0, size), here] = columns[head * size : (head + 1) * size, part]
+
+    def attend(block, group, segments, fresh, lane=0, lanes=QBLOCK):
         queries = pl.ds(pl.multiple_of(block * QBLOCK + lane, LANES), lanes)
         within = pl.ds(lane, lanes)
-        there = pl.ds(start, amount)
-        shade = pl.ds(pl.multiple_of(start - block * QBLOCK, LANES), amount)
-        some = (pl.ds(0, amount), pl.ds(0, lanes))
+        total = sum(amount for _, amount in segments)
+        offsets_at = [sum(amount for _, amount in segments[:i]) for i in range(len(segments))]
+        some = (pl.ds(0, total), pl.ds(0, lanes))
         tops, shrinks = [], []
         for head in range(team):
             low, span = head_window(head, size)
             slot = group * team + head
-            found = jnp.dot(
-                keys[there, pl.ds(pl.multiple_of(group * cols + low, LANES), span)],
-                wide[slot, pl.ds(0, span), queries], preferred_element_type=f32,
-            ) + bias[block, shade, within]
-            scores[(head,) + some] = found
-            tops.append(jnp.max(found, axis=0, keepdims=True))
+            most = None
+            for at, (start, amount) in zip(offsets_at, segments):
+                shade = pl.ds(pl.multiple_of(start - block * QBLOCK, LANES), amount)
+                found = jnp.dot(
+                    keys[pl.ds(start, amount), pl.ds(pl.multiple_of(group * cols + low, LANES), span)],
+                    wide[slot, pl.ds(0, span), queries], preferred_element_type=f32,
+                ) + bias[block, shade, within]
+                scores[head, pl.ds(at, amount), pl.ds(0, lanes)] = found
+                peak = jnp.max(found, axis=0, keepdims=True)
+                most = peak if most is None else jnp.maximum(most, peak)
+            tops.append(most)
         for head in range(team):
             where = block * HEADS + group * team + head
             new = tops[head]
@@ -204,13 +213,19 @@
         for head in range(team):
             slot = group * team + head
             where = block * HEADS + slot
-            mixed = jnp.dot(turned[slot, :, there], probs[(head,) + some], preferred_element_type=f32)
+            mixed = None
+            for at, (start, amount) in zip(offsets_at, segments):
+                part = jnp.dot(
+                    turned[slot, :, pl.ds(start, amount)], probs[head, pl.ds(at, amount), pl.ds(0, lanes)],
+                    preferred_element_type=f32,
+                )
+                mixed = part if mixed is None else mixed + part
             if not fresh:
                 mixed = acc[where, :, within] * shrinks[head] + mixed
             acc[where, :, within] = mixed
 
     own_tokens.wait()
-    norm(MAXLEN, local)
+    norm(MAXLEN, local, MAXLEN)
 
     wide[...] = jnp.zeros(wide.shape, bf16)
     turned[:, pl.ds(size, ONES), :] = jnp.ones((HEADS, ONES, long), bf16)
@@ -272,7 +287,7 @@
             def _():
                 (down if side else up)(hop).wait_recv()
 
-            norm(place(side, hop), HOP)
+            norm(place(side, hop), HOP, place(side, hop) if hop < NEAR else side * HOP)
 
     near = NEAR * HOP
 
@@ -283,18 +298,14 @@
             project_kv(near_starts[side], near, group)
 
     def near_attend(group):
-        @pl.loop(0, 2)
-        def _(side):
-            start = pl.multiple_of(near_starts[0] + side * (near_starts[1] - near_starts[0]), near)
-
-            @pl.loop(0, blocks)
-            def _(block):
-                attend(block, group, start, near, False)
+        @pl.loop(0, blocks)
+        def _(block):
+            attend(block, group, [(start, near) for start in near_starts], False)
 
     def own_attend(group):
         @pl.loop(0, blocks)
         def _(block):
-            attend(block, group, MAXLEN, local, True)
+            attend(block, group, [(MAXLEN, local)], True)
 
     def ready(*chunks):
         for j in chunks:
@@ -306,13 +317,13 @@
 
         @pl.loop(0, GROUPS)
         def _(group):
-            for side in range(2):
-                project_kv(place(side, hop), HOP, group)
+            project_kv(0, 2 * HOP, group, (place(0, hop), place(1, hop)))
             for side in range(2):
                 lanes = min(QBLOCK, (HOPS - hop) * HOP)
-                attend(side * (blocks - 1), group, place(side, hop), HOP, False, side * (QBLOCK - lanes), lanes)
-
-    tile = 256
+                spot = [(place(side, hop), HOP)]
+                attend(side * (blocks - 1), group, spot, False, side * (QBLOCK - lanes), lanes)
+
+    tile = cols
 
     def finish(start, amount):
         for at in range(start, start + amount, HOP):
@@ -328,14 +339,15 @@
 
             context[pl.ds(at, HOP)] = flat[...].T
 
-    def emit(start, amount):
-        where = pl.ds(start, amount)
-
+    def emit(starts, amount):
         @pl.loop(0, width // tile)
         def _(c):
-            at = pl.ds(pl.multiple_of(c * tile, tile), tile)
-            mixed = jnp.dot(context[where], wo_full[:, at], preferred_element_type=f32)
-            hidden[where, at] = (toks[pl.ds(MAXLEN + start, amount), at].astype(f32) + mixed).astype(bf16)
+            at = pl.ds(pl.multiple_of(c * tile, LANES), tile)
+            lhs = jnp.concatenate([context[pl.ds(start, amount)] for start in starts], axis=0)
+            mixed = jnp.dot(lhs, wo_full[:, at], preferred_element_type=f32)
+            for i, start in enumerate(starts):
+                residual = toks[pl.ds(MAXLEN + start, amount), at].astype(f32)
+                hidden[pl.ds(start, amount), at] = (residual + mixed[i * amount : (i + 1) * amount]).astype(bf16)
 
     def relay(j):
         relay_y(j)
@@ -371,12 +383,11 @@
         far(hop)
     ready(*range(WIDE_CHUNKS, CHUNKS))
     finish(HOP, local - 2 * HOP)
-    emit(HOP, local - 2 * HOP)
+    emit((HOP,), local - 2 * HOP)
     far(HOPS - 1)
     for start in (0, local - HOP):
         finish(start, HOP)
-    for start in (0, local - HOP):
-        emit(start, HOP)
+    emit((0, local - HOP), HOP)
 
     sums[...] = jnp.dot(onehot[...], hidden[...], preferred_element_type=f32) / amounts
     for p in range(count):

time: 96.5 us -> 94.2 us (0.976)
  Pallas kernels: 92.5 us -> 90.2 us
    pallas_call x1, Pallas kernels: 92.5 us -> 90.2 us  [shards(): pl.pallas_call(functools.partial(block_kernel, nx, ny), out_shape=(jax.Sh...]
where the time goes in v3:
time: 94.2 us; the launch traced here: 94 us
  Pallas kernels  90.2 us (96%)
  local copies, waits for them, and re-layouts  3.13 us (3%)
    pallas_call x1, Pallas kernels, shards(): pl.pallas_call(functools.partial(block_kernel, nx, ny), out_shape=(jax.Sh...  90.2 us
    unnamed x6, local copies, waits for them, and re-layouts  3.13 us

profile of v3, /device:TPU:0, one launch (start us, length us, event | category | flops | bytes accessed | tf_op | source)
XLA Modules:
  0.0 94.0 jit_solution(13639651088704648071)
XLA Ops:
  0.6 0.0 copy-start
  0.6 0.7 copy-done
  1.3 0.0 copy-start.1
  1.3 0.7 copy-done.1
  2.0 90.2 %block.1 = (bf16[512,1280]{1,0:T(8,128)(2,1)S(1)}, f32[64,1280]{1,0:T(8,128)S(1)}) custom-call(bf16[512,1280]{1,0:T(8,128)(2,1)} %bitcast.7, s32[1,64]{1,0:T(1,128)S(1)} %copy-done.1, f32[10,128]{1,0:T(8,128)S(1)} %bitcast.6, bf16[640,3840]{1,0:T(8,128)(2,1)} %wq.1, bf16[640,1280]{1,0:T(8,128)(2,1)} %wo.1), custom_call_target="tpu_custom_call" | custom-call | tf_op jit(solution)/shard_map/block/pallas_call | solution.py:446
  92.2 1.1 %copy.9 = bf16[1,512,1280]{2,1,0:T(8,128)(2,1)} copy(bf16[1,512,1280]{2,1,0:T(8,128)(2,1)S(1)} %bitcast.4) | data formatting | bytes 2621440
  93.2 0.7 copy.10
Async XLA Ops:
  0.6 0.7 copy-start
  1.3 0.7 copy-start.1

commit v4 on v3

--- a/solution.py
+++ b/solution.py
@@ -384,12 +384,17 @@
     ready(*range(WIDE_CHUNKS, CHUNKS))
     finish(HOP, local - 2 * HOP)
     emit((HOP,), local - 2 * HOP)
+    inner = slice(HOP, local - HOP)
+    sums[...] = jnp.dot(onehot[:, inner], hidden[inner], preferred_element_type=f32)
     far(HOPS - 1)
     for start in (0, local - HOP):
         finish(start, HOP)
     emit((0, local - HOP), HOP)
 
-    sums[...] = jnp.dot(onehot[...], hidden[...], preferred_element_type=f32) / amounts
+    found = sums[...]
+    for edge in (slice(0, HOP), slice(local - HOP, local)):
+        found = found + jnp.dot(onehot[:, edge], hidden[edge], preferred_element_type=f32)
+    sums[...] = found * (1.0 / amounts)
     for p in range(count):
         parts[p] = sums[p * each : (p + 1) * each].astype(bf16)
 

time: 94.2 us -> 94.3 us (level)
  no operation moved by 1% of the time
where the time goes in v4:
time: 94.3 us; the launch traced here: 94.1 us
  Pallas kernels  90.3 us (96%)
  local copies, waits for them, and re-layouts  3.13 us (3%)
    pallas_call x1, Pallas kernels, shards(): pl.pallas_call(functools.partial(block_kernel, nx, ny), out_shape=(jax.Sh...  90.3 us
    unnamed x6, local copies, waits for them, and re-layouts  3.13 us

profile of v4, /device:TPU:0, one launch (start us, length us, event | category | flops | bytes accessed | tf_op | source)
XLA Modules:
  0.0 94.1 jit_solution(14501418526484826385)
XLA Ops:
  0.6 0.0 copy-start
  0.6 0.7 copy-done
  1.3 0.0 copy-start.1
  1.3 0.7 copy-done.1
  2.0 90.3 %block.1 = (bf16[512,1280]{1,0:T(8,128)(2,1)S(1)}, f32[64,1280]{1,0:T(8,128)S(1)}) custom-call(bf16[512,1280]{1,0:T(8,128)(2,1)} %bitcast.7, s32[1,64]{1,0:T(1,128)S(1)} %copy-done.1, f32[10,128]{1,0:T(8,128)S(1)} %bitcast.6, bf16[640,3840]{1,0:T(8,128)(2,1)} %wq.1, bf16[640,1280]{1,0:T(8,128)(2,1)} %wo.1), custom_call_target="tpu_custom_call" | custom-call | tf_op jit(solution)/shard_map/block/pallas_call | solution.py:451
  92.3 1.1 %copy.9 = bf16[1,512,1280]{2,1,0:T(8,128)(2,1)} copy(bf16[1,512,1280]{2,1,0:T(8,128)(2,1)S(1)} %bitcast.4) | data formatting | bytes 2621440
  93.4 0.7 copy.10
Async XLA Ops:
  0.6 0.7 copy-start
  1.3 0.7 copy-start.1
